TPU v7x, 32 devices: a whole 2x2x4 slice. The times are simulated.
32 devices in a mesh: replica: 8 (over z, core), group: 4 (over y, x).
Axes of the slice: x: 2, y: 2, z: 4, core: 2. Of those that a mesh axis runs over, the one named last changes fastest.
Arguments:
- deltas: bfloat16 [2, 8, 3072, 6144], P(None, 'replica', 'group'), may hold values from -8000 to 8000
- master: float32 [2, 3072, 6144], P(None, ('group', 'replica')), may hold values from -6 to 6
- momentum: float32 [2, 3072, 6144], P(None, ('group', 'replica')), may hold values from -6 to 6
Outputs:
- new_master: float32 [2, 3072, 6144], P(None, ('group', 'replica'))
- new_momentum: float32 [2, 3072, 6144], P(None, ('group', 'replica'))
- worker_params: bfloat16 [2, 3072, 6144], P(None, 'group')
All inputs are finite; a program needn't handle non-finite values.
Results may differ from a plain program's by a relative error of at most 0.0065.
Values may be sent and summed in bfloat16 or wider, within the bound.
A program may use at most 128 MiB of HBM per device.

v0:
```python
import jax
import jax.numpy as jnp
from jax import lax
from jax.sharding import PartitionSpec as P

D = 6144
ROWS = 3072


def reduce_together(locals_all, workers):
    summed = lax.psum_scatter(
        locals_all.astype(jnp.float32).astype(jnp.bfloat16),
        "replica",
        scatter_dimension=1,
        tiled=True,
    ).astype(jnp.float32)
    return summed / workers


def update_fragment(averaged, squares, master, momentum):
    factor = jnp.minimum(1.0, 0.25 * jnp.sqrt(float(ROWS * D)) / (jnp.sqrt(squares) + 1e-06))
    clipped = factor * averaged
    moved = 0.9 * momentum + clipped
    updated = master - 0.7 * (clipped + 0.9 * moved)
    return (updated, moved)


def on_device(deltas, master, momentum):
    workers = lax.axis_size("replica")
    frag_count = deltas.shape[0]
    averages = []
    sums_list = []
    joined = reduce_together(deltas[:, 0], workers)
    averages = [joined[frag] for frag in range(frag_count)]
    for frag in range(frag_count):
        averaged = averages[frag]
        sums_list.append(lax.psum(jnp.sum(averaged * averaged), ("replica", "group")))
    masters = []
    moments = []
    shipped = []
    for frag in range(frag_count):
        updated, moved = update_fragment(
            averages[frag], sums_list[frag], master[frag], momentum[frag]
        )
        masters.append(updated)
        moments.append(moved)
        rounded = updated.astype(jnp.bfloat16)
        shipped.append(lax.all_gather(rounded, "replica", axis=0, tiled=True))
    params_out = jnp.stack(shipped)
    return (jnp.stack(masters), jnp.stack(moments), params_out)


def solution(mesh):
    return jax.shard_map(
        on_device,
        mesh=mesh,
        in_specs=(
            P(None, "replica", "group", None),
            P(None, ("group", "replica"), None),
            P(None, ("group", "replica"), None),
        ),
        out_specs=(
            P(None, ("group", "replica"), None),
            P(None, ("group", "replica"), None),
            P(None, "group", None),
        ),
        check_vma=False,
    )
```

profile of v0, /device:TPU:0, one launch (start us, length us, event | category | flops | bytes accessed | tf_op | source)
XLA Modules:
  0.0 457.3 jit_solution(3088841365478419533)
XLA Ops:
  7.2 0.0 reduce-scatter.2.cloned.1.call-start
  7.2 0.7 reduce-scatter.2.cloned.1.call-update
  7.9 0.0 all-gather.3.cloned.1.call-start
  7.9 193.0 %reduce-scatter.2.cloned.1.call-done = bf16[2,96,6144]{2,1,0:T(8,128)(2,1)} async-done(((bf16[2,768,6144]{2,1,0:T(8,128)(2,1)}), bf16[2,96,6144]{2,1,0:T(8,128)(2,1)}) %reduce-scatter.2.cloned.1.call-update) | async-done | bytes 2359312 | tf_op jit(solution)/shard_map/reduce_scatter | solution.py:11
  201.0 2.2 convert_multiply_fusion
  203.2 0.0 copy-start
  203.2 1.6 multiply_reduce_fusion.1
  204.8 0.6 copy-done
  205.4 38.0 %all-reduce = (f32[]{:T(128)}, f32[]{:T(128)}) all-reduce(f32[]{:T(128)} %get-tuple-element.4, f32[]{:T(128)} %get-tuple-element.3), channel_id=1, replica_groups=mesh['replica'=8,'group'=4] {'replica','group'}, use_global_device_ids=true, to_apply=%region_4.0 | all-reduce | flops 2 | bytes 16 | tf_op jit(solution)/shard_map/psum | solution.py:37
  244.8 7.1 %fusion.9 = (bf16[96,6144]{1,0:T(8,128)(2,1)}, bf16[96,6144]{1,0:T(8,128)(2,1)}) fusion(f32[2,96,6144]{2,1,0:T(8,128)} %param.4, f32[2,96,6144]{2,1,0:T(8,128)} %param.5, f32[2,96,6144]{2,1,0:T(8,128)} %copy-done, f32[]{:T(128)S(6)} %min.6, f32[]{:T(128)S(6)} %min.7), kind=kLoop, calls=%fused_computation.15 | loop fusion | flops 9437184 | bytes 16515080 | tf_op jit(solution)/shard_map/convert_element_type | solution.py:47
  251.9 0.0 all-gather.3.cloned.1.call-update
  252.0 0.0 all-gather.5.cloned.1.call-start
  252.0 0.7 all-gather.5.cloned.1.call-update
  252.7 5.7 %multiply_subtract_fusion.1 = (f32[1,96,6144]{2,1,0:T(8,128)S(1)}, f32[1,96,6144]{2,1,0:T(8,128)S(1)}, f32[1,96,6144]{2,1,0:T(8,128)S(1)}, f32[1,96,6144]{2,1,0:T(8,128)S(1)}) fusion(f32[2,96,6144]{2,1,0:T(8,128)} %param.4, f32[2,96,6144]{2,1,0:T(8,128)} %copy-done, f32[]{:T(128)S(6)} %min.6, f32[2,96,6144]{2,1,0:T(8,128)} %param.5, f32[]{:T(128)S(6)} %min.7), kind=kLoop, calls=%fused_computation.19 | loop fusion | flops 8257536 | bytes 23592968 | tf_op jit(solution)/shard_map/sub | solution.py:24
  258.4 5.0 %pad_maximum_fusion.1 = (f32[2,96,6144]{2,1,0:T(8,128)}, f32[2,96,6144]{2,1,0:T(8,128)}) fusion(f32[1,96,6144]{2,1,0:T(8,128)S(1)} %get-tuple-element.13, f32[1,96,6144]{2,1,0:T(8,128)S(1)} %get-tuple-element.7, f32[1,96,6144]{2,1,0:T(8,128)S(1)} %get-tuple-element.14, f32[1,96,6144]{2,1,0:T(8,128)S(1)} %get-tuple-element.8), kind=kLoop, calls=%fused_computation.1 | loop fusion | flops 2359296 | bytes 18874368 | tf_op jit(solution)/shard_map/stack | solution.py:50
  263.4 80.1 %all-gather.3.cloned.1.call-done = bf16[768,6144]{1,0:T(8,128)(2,1)} async-done(((bf16[96,6144]{1,0:T(8,128)(2,1)}), bf16[768,6144]{1,0:T(8,128)(2,1)}) %all-gather.3.cloned.1.call-update) | async-done | bytes 9437200 | tf_op jit(solution)/shard_map/all_gather | solution.py:48
  343.5 90.8 %all-gather.5.cloned.1.call-done = bf16[768,6144]{1,0:T(8,128)(2,1)} async-done(((bf16[96,6144]{1,0:T(8,128)(2,1)}), bf16[768,6144]{1,0:T(8,128)(2,1)}) %all-gather.5.cloned.1.call-update) | async-done | bytes 9437200 | tf_op jit(solution)/shard_map/all_gather | solution.py:48
  434.2 16.5 %pad_maximum_fusion = bf16[2,768,6144]{2,1,0:T(8,128)(2,1)} fusion(bf16[1,768,6144]{2,1,0:T(8,128)(2,1)} %bitcast.37, bf16[1,768,6144]{2,1,0:T(8,128)(2,1)} %bitcast.36), kind=kLoop, calls=%fused_computation | loop fusion | flops 9437184 | bytes 37748736 | tf_op jit(solution)/shard_map/stack | solution.py:49
Async XLA Ops:
  7.2 193.8 %reduce-scatter.2.cloned.1.call-start = ((), (), s32[]{:S(2)}) async-start(), calls=%async_computation.1 | async-start | bytes 21233664 | tf_op jit(solution)/shard_map/reduce_scatter | solution.py:11
  7.9 335.6 %all-gather.3.cloned.1.call-start = ((), (), s32[]{:S(2)}) async-start(), calls=%async_computation.2 | async-start | bytes 10616832 | tf_op jit(solution)/shard_map/all_gather | solution.py:48
  203.2 2.2 copy-start
  252.0 182.3 %all-gather.5.cloned.1.call-start = ((), (), s32[]{:S(2)}) async-start(), calls=%async_computation.3 | async-start | bytes 10616832 | tf_op jit(solution)/shard_map/all_gather | solution.py:48
Sparse Core Ops, SparseCore 0:
  10.3 190.6 reduce-scatter.1
  252.1 91.3 all-gather.2
  345.1 89.1 all-gather.4
where the time goes:
time: 458 us; the launch traced here: 457 us
  waiting for transfers between devices  365 us (80%)
  other arithmetic  38.1 us (8%)
  blocking collectives  38 us (8%)
  between operations  15.2 us (3%)
    reduce_scatter x1, waiting for transfers between devices, reduce_together(): lax.psum_scatter(locals_all.astype(jnp.float32).astype(jnp.bfloat16), 're...  193 us
    all_gather x2, waiting for transfers between devices, on_device(): shipped.append(lax.all_gather(rounded, 'replica', axis=0, tiled=True))  171 us
    psum x1, blocking collectives, on_device(): lax.psum(jnp.sum(averaged * averaged), ('replica', 'group'))  38 us
    another operation x1, other arithmetic, on_device(): params_out = jnp.stack(shipped)  16.5 us
  transfers between devices with their start and end apart: 3, of which 3 were waited for; matrix products, arithmetic and copies ran while one was open for 2% of the time, Pallas kernels for 0%

commit v1 on v0

v1 whole, which is shorter than its diff:
```python
import functools

import jax
import jax.numpy as jnp
from jax import lax
from jax.experimental import pallas as pl
from jax.experimental.pallas import tpu as pltpu
from jax.sharding import PartitionSpec as P

MESH = pl.DeviceIdType.MESH
CORES = 2


def sync_kernel(
    n, groups, width,
    deltas, master, momentum,
    out_master, out_momentum, out_params,
    mine, theirs, arrived, average, mas, mom, params, sq_rows, sq_groups, sq_send,
    load_sem, pair_send, pair_recv, line_send, line_recv,
    right_send, left_send, twin_send, ag_recv, twin_recv,
    keep_sem, state_in, state_out, sq_send_a, sq_recv_a, sq_send_b, sq_recv_b,
):
    frags, m, pieces, rc, depth = mine.shape
    me = lax.axis_index("replica")
    grp = lax.axis_index("group")
    z, c = me // CORES, me % CORES
    twin = z * CORES + (1 - c)
    count = float(n * groups * pieces * rc * depth)

    barrier = pltpu.get_barrier_semaphore()
    for d in range(1, n):
        pl.semaphore_signal(barrier, inc=1, device_id=(lax.rem(me + d, n), grp), device_id_type=MESH)
    for d in range(1, groups):
        pl.semaphore_signal(barrier, inc=1, device_id=(me, lax.rem(grp + d, groups)), device_id_type=MESH)
    pl.semaphore_wait(barrier, n + groups - 2)

    def remote(src, dst, send, recv, replica, group=grp):
        return pltpu.make_async_remote_copy(
            src_ref=src, dst_ref=dst, send_sem=send, recv_sem=recv,
            device_id=(replica, group), device_id_type=MESH,
        )

    def load(f, o, k):
        return pltpu.make_async_copy(deltas.at[f, o * CORES + c, k], mine.at[f, o, k], load_sem.at[f, o, k])

    def pair(f, o, k):
        return remote(
            deltas.at[f, o * CORES + (1 - c), k], theirs.at[f, o, k],
            pair_send.at[f, o, k], pair_recv.at[f, o, k], twin,
        )

    def line(f, o, k, slot, to):
        return remote(
            mine.at[f, o, k], arrived.at[f, slot, k], line_send.at[f, o, k], line_recv.at[f, slot, k], to
        )

    def each_piece(body):
        def step(k, carry):
            body(k)
            return carry
        lax.fori_loop(0, pieces, step, 0)

    def each_column(body, init=0):
        def step(j, carry):
            return body(pl.ds(pl.multiple_of(j * width, width), width), carry)
        return lax.fori_loop(0, depth // width, step, init)

    def state(f):
        return (
            pltpu.make_async_copy(master.at[f], mas.at[f], state_in.at[0, f]),
            pltpu.make_async_copy(momentum.at[f], mom.at[f], state_in.at[1, f]),
        )

    def state_back(f):
        return (
            pltpu.make_async_copy(mas.at[f], out_master.at[f], state_out.at[0, f]),
            pltpu.make_async_copy(mom.at[f], out_momentum.at[f], state_out.at[1, f]),
        )

    def by_distance(s, body):
        @pl.when(z + s < m)
        def _():
            body(z + s, 1)

        if s > 0:
            @pl.when(z - s >= 0)
            def _():
                body(z - s, -1)

    def fetch(f):
        for s in range(m - 1, -1, -1):
            def go(k):
                def one(o, way):
                    load(f, o, k).start()
                    pair(f, o, k).start()
                by_distance(s, one)
            each_piece(go)
        for copy in state(f):
            copy.start()

    def add_pair(f, o, k, cols):
        return mine[f, o, k, :, cols].astype(jnp.float32) + theirs[f, o, k, :, cols].astype(jnp.float32)

    def reduce_far(f, s):
        def go(k):
            def one(o, way):
                load(f, o, k).wait()
                pair(f, o, k).wait_recv()
                to = me + way * CORES
                back = z - way
                inner = (back >= 0) & (back < m)

                @pl.when(inner)
                def _():
                    line(f, o, k, o, to).wait_recv()

                    def body(cols, carry):
                        total = add_pair(f, o, k, cols) + arrived[f, o, k, :, cols].astype(jnp.float32)
                        mine[f, o, k, :, cols] = total.astype(jnp.bfloat16)
                        return carry
                    each_column(body)

                @pl.when(jnp.logical_not(inner))
                def _():
                    def body(cols, carry):
                        mine[f, o, k, :, cols] = add_pair(f, o, k, cols).astype(jnp.bfloat16)
                        return carry
                    each_column(body)

                if s == 1 and way == -1:
                    line(f, o, k, m, to).start()
                else:
                    line(f, o, k, o, to).start()
            by_distance(s, one)
        each_piece(go)

    def reduce_own(f):
        def go(k):
            load(f, z, k).wait()
            pair(f, z, k).wait_recv()

            def start(cols, carry):
                average[f, k, :, cols] = add_pair(f, z, k, cols)
                return carry
            each_column(start)

            for slot, there in ((z, z > 0), (m, z < m - 1)):
                @pl.when(there)
                def _(slot=slot):
                    line(f, z, k, slot, twin).wait_recv()

                    def body(cols, carry):
                        average[f, k, :, cols] += arrived[f, slot, k, :, cols].astype(jnp.float32)
                        return carry
                    each_column(body)
        each_piece(go)

        def piece_squares(k, total):
            def body(cols, total):
                value = average[f, k, :, cols] * (1.0 / n)
                average[f, k, :, cols] = value
                square = value * value
                for r in range(0, rc, 8):
                    for q in range(0, width, 128):
                        total = total + square[r:r + 8, q:q + 128]
                return total
            return each_column(body, total)
        total = lax.fori_loop(0, pieces, piece_squares, jnp.zeros((8, 128), jnp.float32))
        sq_send[f, 0] = total
        sq_rows[f, me] = total
        for d in range(1, n):
            squares_a(f, me, lax.rem(me + d, n), d).start()

    def squares_a(f, slot, to, d):
        return remote(sq_send.at[f, 0], sq_rows.at[f, slot], sq_send_a.at[f, d], sq_recv_a.at[f, slot], to)

    def squares_b(f, slot, to, d):
        return remote(sq_send.at[f, 1], sq_groups.at[f, slot], sq_send_b.at[f, d], sq_recv_b.at[f, slot], me, to)

    def factor_of(f):
        for d in range(1, n):
            squares_a(f, lax.rem(me + d, n), lax.rem(me + d, n), d).wait_recv()
        total = sq_rows[f, 0]
        for r in range(1, n):
            total = total + sq_rows[f, r]
        sq_send[f, 1] = total
        sq_groups[f, grp] = total
        for d in range(1, groups):
            squares_b(f, grp, lax.rem(grp + d, groups), d).start()
        for d in range(1, groups):
            squares_b(f, lax.rem(grp + d, groups), lax.rem(grp + d, groups), d).wait_recv()
        total = sq_groups[f, 0]
        for r in range(1, groups):
            total = total + sq_groups[f, r]
        squares = jnp.sum(jnp.sum(total, axis=1, keepdims=True), axis=0, keepdims=True)
        bound = 0.25 * count ** 0.5
        return jnp.minimum(1.0, bound / (jnp.sqrt(squares) + 1e-06))

    def keep(f, k):
        return pltpu.make_async_copy(params.at[f, k], out_params.at[f, me, k], keep_sem.at[f, k])

    def place(f, o, k):
        return out_params.at[f, o * CORES + c, k]

    def send_right(f, o, k, src):
        return remote(src, place(f, o, k), right_send.at[f, o, k], ag_recv.at[f, o, k], me + CORES)

    def send_left(f, o, k, src):
        return remote(src, place(f, o, k), left_send.at[f, o, k], ag_recv.at[f, o, k], me - CORES)

    def send_twin(f, o, k, src):
        return remote(src, place(f, o, k), twin_send.at[f, o, k], twin_recv.at[f, o, k], twin)

    def update(f):
        factor = factor_of(f)
        for copy in state(f):
            copy.wait()

        def go(k):
            def body(cols, carry):
                clipped = factor * average[f, k, :, cols]
                moved = 0.9 * mom[f, k, :, cols] + clipped
                updated = mas[f, k, :, cols] - 0.7 * (clipped + 0.9 * moved)
                mom[f, k, :, cols] = moved
                mas[f, k, :, cols] = updated
                params[f, k, :, cols] = updated.astype(jnp.bfloat16)
                return carry
            each_column(body)

            @pl.when(z < m - 1)
            def _():
                send_right(f, z, k, params.at[f, k]).start()

            @pl.when(z > 0)
            def _():
                send_left(f, z, k, params.at[f, k]).start()
            send_twin(f, z, k, params.at[f, k]).start()
            keep(f, k).start()
        each_piece(go)
        for copy in state_back(f):
            copy.start()

    def spread(f, s):
        def go(k):
            def one(o, way):
                src = place(f, o, k)
                send_right(f, o, k, src).wait_recv()
                if way == 1:
                    @pl.when(z > 0)
                    def _():
                        send_left(f, o, k, src).start()
                else:
                    @pl.when(z < m - 1)
                    def _():
                        send_right(f, o, k, src).start()
                send_twin(f, o, k, src).start()
            by_distance(s, one)
        each_piece(go)

    def finish(f):
        def go(k):
            def every(o, carry):
                pair(f, o, k).wait_send()
                src = place(f, o, k)
                send_twin(f, o, k, src).wait_send()
                remote(
                    src, out_params.at[f, o * CORES + (1 - c), k],
                    twin_send.at[f, o, k], twin_recv.at[f, o, k], twin,
                ).wait_recv()

                @pl.when(o != z)
                def _():
                    line(f, o, k, o, twin).wait_send()

                @pl.when((z < m - 1) & (o <= z))
                def _():
                    send_right(f, o, k, src).wait_send()

                @pl.when((z > 0) & (o >= z))
                def _():
                    send_left(f, o, k, src).wait_send()
                return carry
            lax.fori_loop(0, m, every, 0)
            keep(f, k).wait()
        each_piece(go)
        for d in range(1, n):
            squares_a(f, me, twin, d).wait_send()
        for d in range(1, groups):
            squares_b(f, grp, lax.rem(grp + d, groups), d).wait_send()
        for copy in state_back(f):
            copy.wait()

    for f in range(frags):
        fetch(f)
    for s in range(m - 1, 0, -1):
        reduce_far(0, s)
    reduce_own(0)
    for f in range(frags):
        if f + 1 < frags:
            reduce_far(f + 1, m - 1)
        update(f)
        for s in range(1, m):
            if f + 1 < frags and m - 1 - s > 0:
                reduce_far(f + 1, m - 1 - s)
            if f + 1 < frags and s == m - 1:
                reduce_own(f + 1)
            spread(f, s)
    for f in range(frags):
        finish(f)


def on_device(deltas, master, momentum):
    n, groups = lax.axis_size("replica"), lax.axis_size("group")
    frags, rows, depth = master.shape
    m = n // CORES
    pieces = 3 if rows % 24 == 0 else 1
    rc = rows // pieces
    width = 512 if depth % 512 == 0 else 128
    state = (frags, pieces, rc, depth)
    dma = pltpu.SemaphoreType.DMA
    per_block = dma((frags, m, pieces))
    hbm = pl.BlockSpec(memory_space=pl.ANY)
    new_master, new_momentum, params = pl.pallas_call(
        functools.partial(sync_kernel, n, groups, width),
        out_shape=(
            jax.ShapeDtypeStruct(state, jnp.float32),
            jax.ShapeDtypeStruct(state, jnp.float32),
            jax.ShapeDtypeStruct((frags, n, pieces, rc, depth), jnp.bfloat16),
        ),
        in_specs=[hbm] * 3,
        out_specs=(hbm,) * 3,
        scratch_shapes=[
            pltpu.VMEM((frags, m, pieces, rc, depth), jnp.bfloat16),
            pltpu.VMEM((frags, m, pieces, rc, depth), jnp.bfloat16),
            pltpu.VMEM((frags, m + 1, pieces, rc, depth), jnp.bfloat16),
            pltpu.VMEM(state, jnp.float32),
            pltpu.VMEM(state, jnp.float32),
            pltpu.VMEM(state, jnp.float32),
            pltpu.VMEM(state, jnp.bfloat16),
            pltpu.VMEM((frags, n, 8, 128), jnp.float32),
            pltpu.VMEM((frags, groups, 8, 128), jnp.float32),
            pltpu.VMEM((frags, 2, 8, 128), jnp.float32),
            per_block, per_block, per_block, per_block, dma((frags, m + 1, pieces)),
            per_block, per_block, per_block, per_block, per_block,
            dma((frags, pieces)), dma((2, frags)), dma((2, frags)),
            dma((frags, n)), dma((frags, n)), dma((frags, groups)), dma((frags, groups)),
        ],
        compiler_params=pltpu.CompilerParams(
            collective_id=0, has_side_effects=True, vmem_limit_bytes=62 * 1024 * 1024
        ),
    )(
        deltas.reshape(frags, n, pieces, rc, depth),
        master.reshape(state),
        momentum.reshape(state),
    )
    return (
        new_master.reshape(master.shape),
        new_momentum.reshape(master.shape),
        params.reshape(frags, n * rows, depth),
    )


def solution(mesh):
    return jax.shard_map(
        on_device,
        mesh=mesh,
        in_specs=(
            P(None, "replica", "group", None),
            P(None, ("group", "replica"), None),
            P(None, ("group", "replica"), None),
        ),
        out_specs=(
            P(None, ("group", "replica"), None),
            P(None, ("group", "replica"), None),
            P(None, "group", None),
        ),
        check_vma=False,
    )
```

time: 458 us -> 304 us (0.66)
  waiting for transfers between devices: 365 us -> 0 us
  Pallas kernels: 0 us -> 283 us
  other arithmetic: 38.1 us -> 0 us
  blocking collectives: 38 us -> 0 us
  local copies, waits for them, and re-layouts: 0.57 us -> 19.5 us
  between operations: 15.2 us -> 0.65 us
    pallas_call x0 -> x1, Pallas kernels: none -> 283 us  [on_device(): pl.pallas_call(functools.partial(sync_kernel, n, groups, width), out_shap...]
    reduce_scatter x1 -> x0, waiting for transfers between devices: 193 us -> none  [reduce_together(): lax.psum_scatter(locals_all.astype(jnp.float32).astype(jnp.bfloat16), 're...]
    all_gather x2 -> x0, waiting for transfers between devices: 171 us -> none  [on_device(): shipped.append(lax.all_gather(rounded, 'replica', axis=0, tiled=True))]
    psum x1 -> x0, blocking collectives: 38 us -> none  [on_device(): lax.psum(jnp.sum(averaged * averaged), ('replica', 'group'))]
    another operation x2 -> x0, other arithmetic: 21.5 us -> none  [the longest x1 16.5 us: on_device(): params_out = jnp.stack(shipped)]
    unnamed x2 -> x5, local copies, waits for them, and re-layouts: 0.57 us -> 19.5 us
    convert_element_type x1 -> x0, other arithmetic: 7.1 us -> none  [on_device(): rounded = updated.astype(jnp.bfloat16)]
    sub x1 -> x0, other arithmetic: 5.69 us -> none  [update_fragment(): updated = master - 0.7 * (clipped + 0.9 * moved)]
  transfers between devices with their start and end apart: 3 -> 0, of which waited for: 3 -> 0; matrix products, arithmetic and copies ran while one was open for 2% -> 0% of each run, Pallas kernels for 0% -> 0%
where the time goes in v1:
time: 304 us
  Pallas kernels  283 us (93%)
  local copies, waits for them, and re-layouts  19.5 us (6%)
    pallas_call x1, Pallas kernels, on_device(): pl.pallas_call(functools.partial(sync_kernel, n, groups, width), out_shap...  283 us
    unnamed x5, local copies, waits for them, and re-layouts  19.5 us

profile of v1, /device:TPU:0, one launch (start us, length us, event | category | flops | bytes accessed | tf_op | source)
XLA Modules:
  0.0 303.5 jit_solution(8862372280808932295)
XLA Ops:
  0.6 283.4 %shard_map.58 = (f32[2,3,32,6144]{3,2,1,0:T(8,128)}, f32[2,3,32,6144]{3,2,1,0:T(8,128)}, bf16[2,8,3,32,6144]{4,3,2,1,0:T(8,128)(2,1)}) custom-call(bf16[2,8,3,32,6144]{4,3,2,1,0:T(8,128)(2,1)} %bitcast.6, f32[2,3,32,6144]{3,2,1,0:T(8,128)} %bitcast.8, f32[2,3,32,6144]{3,2,1,0:T(8,128)} %bitcast.9), custom_call_target="tpu_custom_call" | custom-call | tf_op jit(solution)/shard_map/pallas_call | solution.py:323
  284.1 0.0 copy-start
  284.1 5.3 %copy.9 = f32[2,96,6144]{2,1,0:T(8,128)} copy(f32[2,96,6144]{2,1,0:T(8,128)} %bitcast.11) | data formatting | bytes 9437184
  289.4 5.9 %copy.10 = f32[2,96,6144]{2,1,0:T(8,128)} copy(f32[2,96,6144]{2,1,0:T(8,128)} %bitcast.10) | data formatting | bytes 9437184
  295.4 1.3 copy-done
  296.7 6.8 %copy.11 = bf16[2,768,6144]{2,1,0:T(8,128)(2,1)} copy(bf16[2,768,6144]{2,1,0:T(8,128)(2,1)S(1)} %bitcast.7) | data formatting | bytes 37748736
Async XLA Ops:
  284.1 12.6 %copy-start = (bf16[2,8,3,32,6144]{4,3,2,1,0:T(8,128)(2,1)S(1)}, bf16[2,8,3,32,6144]{4,3,2,1,0:T(8,128)(2,1)}, u32[]{:S(2)}) copy-start(bf16[2,8,3,32,6144]{4,3,2,1,0:T(8,128)(2,1)} %get-tuple-element.8) | copy-start | bytes 56623108
